TPU v7x, 32 devices: a whole 2x2x4 slice. The times are simulated.
32 devices in a mesh: rows: 8 (over y, x, core), feat: 4 (over z).
Axes of the slice: x: 2, y: 2, z: 4, core: 2. Of those that a mesh axis runs over, the one named last changes fastest.
Arguments:
- bins: int32 [8192, 512], P('rows', 'feat'), may hold values from -2147483648 to 2147483647, as said below
- hessian: float32 [32768], P('rows'), may hold values from 0.05 to 1
- thresholds: float32 [128], replicated, may hold values from 0.02 to 0.98
Outputs:
- cuts: float32 [512, 128], P('feat')
Inputs may be any that keep to these rules, and one draw needn't show every extreme that they name: `bins`: each word holds the bin ids, 0 to 255, of rows 4i to 4i + 3 of one feature, row 4i + k in bits 8k to 8k + 7 of the two's complement word.
All inputs are finite; a program needn't handle non-finite values.
Results may differ from a plain program's by a relative error of at most 0.000065.
Values sent between devices are 32-bit elements; how exact they have to be, the bound alone decides.
A program may use at most 192 MiB of HBM per device.

v0:
```python
import math
import jax
import jax.numpy as jnp
from jax import lax
from jax.sharding import PartitionSpec as P

BINS = 256


def unpack(words):
    parts = [jnp.bitwise_and(jnp.right_shift(words, 8 * k), 255) for k in range(4)]
    stacked = jnp.stack(parts, axis=1)
    return stacked.reshape(words.shape[0] * 4, words.shape[1])


def histogram(columns, weights):
    count, width = columns.shape
    limit = max(8, 1048576 // (width * 16))
    block = math.gcd(count, limit)
    col_blocks = columns.reshape(count // block, block, width)
    wt_blocks = weights.reshape(count // block, block)
    levels = jnp.arange(16, dtype=jnp.int32)

    def add_block(total, item):
        col_part, wt_part = item
        high = jnp.right_shift(col_part, 4)
        low = jnp.bitwise_and(col_part, 15)
        high_hot = jnp.where(high[:, :, None] == levels, wt_part[:, None, None], 0.0)
        low_hot = (low[:, :, None] == levels).astype(jnp.float32)
        joint = jnp.einsum("rkh,rkl->khl", high_hot, low_hot, precision=lax.Precision.HIGHEST)
        return (total + joint, None)

    start = jnp.zeros((width, 16, 16), jnp.float32)
    total, unused = lax.scan(add_block, start, (col_blocks, wt_blocks))
    return total.reshape(width, BINS)


def cut_positions(hist, thresholds):
    cum = jnp.cumsum(hist, axis=1)
    before = cum - hist
    total = cum[:, -1]
    target = thresholds[None, :, None] * total[:, None, None]
    ratio = (target - before[:, None, :]) / (hist[:, None, :] + 1.0)
    return jnp.sum(jnp.clip(ratio, 0.0, 1.0), axis=2)


def local(bins, hessian, thresholds):
    regrouped = lax.all_to_all(bins, "rows", split_axis=1, concat_axis=0, tiled=True)
    weights = lax.all_gather(hessian, "rows", axis=0, tiled=True)
    hist = histogram(unpack(regrouped), weights)
    cuts = cut_positions(hist, thresholds)
    return lax.all_gather(cuts, "rows", axis=0, tiled=True)


def solution(mesh):
    in_specs = (P("rows", "feat"), P("rows"), P())
    out_specs = P("feat", None)
    return jax.shard_map(local, mesh=mesh, in_specs=in_specs, out_specs=out_specs, check_vma=False)
```

profile of v0, /device:TPU:0, one launch (start us, length us, event | category | flops | bytes accessed | tf_op | source)
XLA Modules:
  0.0 84.6 jit_solution(17974510913110473244)
XLA Ops:
  0.0 0.0 copy-start
  0.0 2.0 %copy.34 = s32[1024,128]{0,1:T(8,128)} copy(s32[1024,128]{1,0:T(8,128)} %param.5) | data formatting | bytes 1048576 | tf_op args[0]
  2.0 5.2 %all-to-all-start = ((s32[1024,8,16]{0,2,1:T(8,128)}), s32[1024,8,16]{0,2,1:T(8,128)S(1)}, u32[]{:S(2)}, u32[]{:S(2)}) async-start(s32[1024,8,16]{0,2,1:T(8,128)} %bitcast), calls=%async_computation | async-start | bytes 1048576 | tf_op jit(solution)/shard_map/all_to_all | solution.py:48
  7.2 0.0 copy-done
  7.3 13.2 %all_gather.6 = f32[32768]{0:T(1024)S(1)} all-gather(f32[4096]{0:T(1024)S(1)} %copy-done), channel_id=1, replica_groups=mesh['rows'=8,'feat'=4] {'rows'}, dimensions={0}, use_global_device_ids=true | all-gather | bytes 147456 | tf_op jit(solution)/shard_map/all_gather | solution.py:49
  20.5 0.0 all-to-all-done
  20.5 0.3 and_bitcast_fusion.4
  20.7 0.3 copy.35
  21.1 0.1 and.76
  21.2 0.3 copy.36
  21.5 0.1 and.79
  21.6 0.3 copy.37
  21.9 0.9 %and.82 = s32[8192,1,16]{0,2,1:T(8,128)} reshape(s32[8,1024,16]{1,0,2:T(8,128)S(1)} %copy.37) | data formatting | bytes 1048576 | tf_op jit(solution)/shard_map/and | solution.py:11
  22.8 0.3 copy.38
  23.1 0.9 %and.85 = s32[8192,1,16]{0,2,1:T(8,128)} reshape(s32[8,1024,16]{1,0,2:T(8,128)S(1)} %copy.38) | data formatting | bytes 1048576 | tf_op jit(solution)/shard_map/and | solution.py:11
  24.0 1.3 %pad_add_fusion = s32[8192,4,16]{0,2,1:T(8,128)S(1)} fusion(s32[8192,1,16]{0,2,1:T(8,128)} %and.85, s32[8192,1,16]{0,2,1:T(8,128)} %and.82, s32[8192,1,16]{0,2,1:T(8,128)S(1)} %and.79, s32[8192,1,16]{0,2,1:T(8,128)S(1)} %and.76), kind=kLoop, calls=%fused_computation.14 | loop fusion | flops 1572864 | bytes 4194304 | tf_op jit(solution)/shard_map/stack | solution.py:12
  25.4 10.7 %copy.39 = s32[8192,4,16]{2,1,0:T(4,128)} copy(s32[8192,4,16]{0,2,1:T(8,128)S(1)} %pad_add_fusion) | data formatting | bytes 4194304 | tf_op jit(solution)/shard_map/stack | solution.py:12
  36.1 9.6 %copy.40 = s32[8,4096,16]{1,2,0:T(8,128)S(1)} copy(s32[8,4096,16]{2,1,0:T(8,128)} %bitcast.35) | data formatting | bytes 4194304
  45.7 0.0 copy-start.1
  45.7 27.9 %while.12 = (s32[]{:T(128)}, f32[16,16,16]{2,1,0:T(8,128)S(1)}, s32[8,4096,16]{1,2,0:T(8,128)S(1)}, f32[8,4096]{1,0:T(8,128)S(1)}, s32[]{:T(128)}, /*index=5*/s32[]{:T(128)}) while((s32[]{:T(128)}, f32[16,16,16]{2,1,0:T(8,128)S(1)}, s32[8,4096,16]{1,2,0:T(8,128)S(1)}, f32[8,4096]{1,0:T(8,128)S(1)}, s32[]{:T(128)}, ...), condition=%wide.region_1.2_spmd.clone.clone, body=%wide.region_0.1_spmd.clone.clone.sunk | while | flops 204611584 | bytes 1392727 | solution.py:34
  45.8 3.4 %fusion.16 = f32[16,16,16]{2,1,0:T(8,128)S(1)} fusion(s32[4096,16]{0,1:T(8,128)S(1)} %get-tuple-element.126, f32[4096]{0:T(1024)S(1)} %bitcast.36, s32[4096,16]{0,1:T(8,128)S(1)} %get-tuple-element.127, f32[16,16,16]{2,1,0:T(8,128)S(1)} %get-tuple-element.135, pred[]{:T(512)S(6)} %compare.3), kind=kOutput, calls=%fused_computation.9.clone.1 | convolution fusion | flops 204480512 | bytes 573441 | tf_op jit(solution)/shard_map/while/body/eval_jaxpr/rkh,rkl->khl/dot_general | solution.py:30
  49.3 3.4 %fusion.16 = f32[16,16,16]{2,1,0:T(8,128)S(1)} fusion(s32[4096,16]{0,1:T(8,128)S(1)} %get-tuple-element.126, f32[4096]{0:T(1024)S(1)} %bitcast.36, s32[4096,16]{0,1:T(8,128)S(1)} %get-tuple-element.127, f32[16,16,16]{2,1,0:T(8,128)S(1)} %get-tuple-element.135, pred[]{:T(512)S(6)} %compare.3), kind=kOutput, calls=%fused_computation.9.clone.1 | convolution fusion | flops 204480512 | bytes 573441 | tf_op jit(solution)/shard_map/while/body/eval_jaxpr/rkh,rkl->khl/dot_general | solution.py:30
  52.8 3.4 %fusion.16 = f32[16,16,16]{2,1,0:T(8,128)S(1)} fusion(s32[4096,16]{0,1:T(8,128)S(1)} %get-tuple-element.126, f32[4096]{0:T(1024)S(1)} %bitcast.36, s32[4096,16]{0,1:T(8,128)S(1)} %get-tuple-element.127, f32[16,16,16]{2,1,0:T(8,128)S(1)} %get-tuple-element.135, pred[]{:T(512)S(6)} %compare.3), kind=kOutput, calls=%fused_computation.9.clone.1 | convolution fusion | flops 204480512 | bytes 573441 | tf_op jit(solution)/shard_map/while/body/eval_jaxpr/rkh,rkl->khl/dot_general | solution.py:30
  56.2 3.4 %fusion.16 = f32[16,16,16]{2,1,0:T(8,128)S(1)} fusion(s32[4096,16]{0,1:T(8,128)S(1)} %get-tuple-element.126, f32[4096]{0:T(1024)S(1)} %bitcast.36, s32[4096,16]{0,1:T(8,128)S(1)} %get-tuple-element.127, f32[16,16,16]{2,1,0:T(8,128)S(1)} %get-tuple-element.135, pred[]{:T(512)S(6)} %compare.3), kind=kOutput, calls=%fused_computation.9.clone.1 | convolution fusion | flops 204480512 | bytes 573441 | tf_op jit(solution)/shard_map/while/body/eval_jaxpr/rkh,rkl->khl/dot_general | solution.py:30
  59.7 3.4 %fusion.16 = f32[16,16,16]{2,1,0:T(8,128)S(1)} fusion(s32[4096,16]{0,1:T(8,128)S(1)} %get-tuple-element.126, f32[4096]{0:T(1024)S(1)} %bitcast.36, s32[4096,16]{0,1:T(8,128)S(1)} %get-tuple-element.127, f32[16,16,16]{2,1,0:T(8,128)S(1)} %get-tuple-element.135, pred[]{:T(512)S(6)} %compare.3), kind=kOutput, calls=%fused_computation.9.clone.1 | convolution fusion | flops 204480512 | bytes 573441 | tf_op jit(solution)/shard_map/while/body/eval_jaxpr/rkh,rkl->khl/dot_general | solution.py:30
  63.2 3.4 %fusion.16 = f32[16,16,16]{2,1,0:T(8,128)S(1)} fusion(s32[4096,16]{0,1:T(8,128)S(1)} %get-tuple-element.126, f32[4096]{0:T(1024)S(1)} %bitcast.36, s32[4096,16]{0,1:T(8,128)S(1)} %get-tuple-element.127, f32[16,16,16]{2,1,0:T(8,128)S(1)} %get-tuple-element.135, pred[]{:T(512)S(6)} %compare.3), kind=kOutput, calls=%fused_computation.9.clone.1 | convolution fusion | flops 204480512 | bytes 573441 | tf_op jit(solution)/shard_map/while/body/eval_jaxpr/rkh,rkl->khl/dot_general | solution.py:30
  66.7 3.4 %fusion.16 = f32[16,16,16]{2,1,0:T(8,128)S(1)} fusion(s32[4096,16]{0,1:T(8,128)S(1)} %get-tuple-element.126, f32[4096]{0:T(1024)S(1)} %bitcast.36, s32[4096,16]{0,1:T(8,128)S(1)} %get-tuple-element.127, f32[16,16,16]{2,1,0:T(8,128)S(1)} %get-tuple-element.135, pred[]{:T(512)S(6)} %compare.3), kind=kOutput, calls=%fused_computation.9.clone.1 | convolution fusion | flops 204480512 | bytes 573441 | tf_op jit(solution)/shard_map/while/body/eval_jaxpr/rkh,rkl->khl/dot_general | solution.py:30
  70.2 3.4 %fusion.16 = f32[16,16,16]{2,1,0:T(8,128)S(1)} fusion(s32[4096,16]{0,1:T(8,128)S(1)} %get-tuple-element.126, f32[4096]{0:T(1024)S(1)} %bitcast.36, s32[4096,16]{0,1:T(8,128)S(1)} %get-tuple-element.127, f32[16,16,16]{2,1,0:T(8,128)S(1)} %get-tuple-element.135, pred[]{:T(512)S(6)} %compare.3), kind=kOutput, calls=%fused_computation.9.clone.1 | convolution fusion | flops 204480512 | bytes 573441 | tf_op jit(solution)/shard_map/while/body/eval_jaxpr/rkh,rkl->khl/dot_general | solution.py:30
  73.6 0.1 reshape.161
  73.7 0.1 reshape.163
  73.8 0.6 reduce-window.6
  74.4 0.2 slice_reduce_fusion
  74.6 0.1 copy_bitcast_fusion
  74.7 0.1 fusion.12
  74.8 0.2 slice_reduce_fusion.1
  75.0 0.0 copy-done.1
  75.0 0.1 broadcast_multiply_fusion
  75.0 0.7 clamp_reduce_fusion
  75.7 8.3 %all_gather.7 = f32[128,128]{1,0:T(8,128)S(1)} all-gather(f32[16,128]{1,0:T(8,128)S(1)} %clamp_reduce_fusion), channel_id=1, replica_groups=mesh['rows'=8,'feat'=4] {'rows'}, dimensions={0}, use_global_device_ids=true | all-gather | bytes 73728 | tf_op jit(solution)/shard_map/all_gather | solution.py:52
  84.0 0.6 copy.54
  (21 shorter events, 0.6 us)
Async XLA Ops:
  0.0 7.2 %copy-start = (f32[4096]{0:T(1024)S(1)}, f32[4096]{0:T(1024)}, u32[]{:S(2)}) copy-start(f32[4096]{0:T(1024)} %param.6) | copy-start | bytes 49156
  2.0 18.4 %all-to-all-start = ((s32[1024,8,16]{0,2,1:T(8,128)}), s32[1024,8,16]{0,2,1:T(8,128)S(1)}, u32[]{:S(2)}, u32[]{:S(2)}) async-start(s32[1024,8,16]{0,2,1:T(8,128)} %bitcast), calls=%async_computation | async-start | bytes 1048576 | tf_op jit(solution)/shard_map/all_to_all | solution.py:48
  45.7 29.3 %copy-start.1 = (f32[128]{0:T(128)S(1)}, f32[128]{0:T(128)}, u32[]{:S(2)}) copy-start(f32[128]{0:T(128)} %param.7) | copy-start | bytes 1540
where the time goes:
time: 85 us; the launch traced here: 84.6 us
  matrix products  27.1 us (32%)
  local copies, waits for them, and re-layouts  27 us (32%)
  blocking collectives  21.5 us (25%)
  starting transfers between devices  5.2 us (6%)
  other arithmetic  3.46 us (4%)
    dot_general x8, matrix products, add_block(): jnp.einsum('rkh,rkl->khl', high_hot, low_hot, precision=lax.Precision.HIG...  27.1 us
    all_gather x1, blocking collectives, local(): weights = lax.all_gather(hessian, 'rows', axis=0, tiled=True)  13.2 us
    unnamed x7, local copies, waits for them, and re-layouts  12.3 us
    another operation x1, local copies, waits for them, and re-layouts, unpack(): stacked = jnp.stack(parts, axis=1)  10.7 us
    all_gather x1, blocking collectives, local(): return lax.all_gather(cuts, 'rows', axis=0, tiled=True)  8.29 us
    all_to_all x1, starting transfers between devices, local(): lax.all_to_all(bins, 'rows', split_axis=1, concat_axis=0, tiled=True)  5.2 us
    and x8, local copies, waits for them, and re-layouts, unpack(): jnp.bitwise_and(jnp.right_shift(words, 8 * k), 255)  3.23 us
  transfers between devices with their start and end apart: 1, of which 0 were waited for; matrix products, arithmetic and copies ran while one was open for 0% of the time, Pallas kernels for 0%

commit v1 on v0

--- a/solution.py
+++ b/solution.py
@@ -45,7 +45,13 @@
 
 
 def local(bins, hessian, thresholds):
-    regrouped = lax.all_to_all(bins, "rows", split_axis=1, concat_axis=0, tiled=True)
+
+    def figure_plan(mine_x):
+        return jnp.concatenate(
+            lax.all_to_all(jnp.stack(jnp.split(mine_x, lax.axis_size("rows"), 1)), "rows", 0, 0), 0
+        )
+
+    regrouped = figure_plan(bins)
     weights = lax.all_gather(hessian, "rows", axis=0, tiled=True)
     hist = histogram(unpack(regrouped), weights)
     cuts = cut_positions(hist, thresholds)

time: 85 us -> 96.5 us (1.14)
  local copies, waits for them, and re-layouts: 27 us -> 38.4 us
    unnamed x7 -> x21, local copies, waits for them, and re-layouts: 12.3 us -> 18.1 us
    split x0 -> x1, local copies, waits for them, and re-layouts: none -> 5.01 us  [figure_plan(): jnp.split(mine_x, lax.axis_size('rows'), 1)]
where the time goes in v1:
time: 96.5 us; the launch traced here: 96.1 us
  local copies, waits for them, and re-layouts  38.4 us (40%)
  matrix products  27.1 us (28%)
  blocking collectives  21.5 us (22%)
  starting transfers between devices  5.2 us (5%)
  other arithmetic  3.47 us (4%)
    dot_general x8, matrix products, add_block(): jnp.einsum('rkh,rkl->khl', high_hot, low_hot, precision=lax.Precision.HIG...  27.1 us
    unnamed x21, local copies, waits for them, and re-layouts  18.1 us
    all_gather x1, blocking collectives, local(): weights = lax.all_gather(hessian, 'rows', axis=0, tiled=True)  13.2 us
    another operation x1, local copies, waits for them, and re-layouts, unpack(): stacked = jnp.stack(parts, axis=1)  10.7 us
    all_gather x1, blocking collectives, local(): return lax.all_gather(cuts, 'rows', axis=0, tiled=True)  8.29 us
    all_to_all x1, starting transfers between devices, figure_plan(): lax.all_to_all(jnp.stack(jnp.split(mine_x, lax.axis_size('rows'), 1)), 'r...  5.2 us
    split x1, local copies, waits for them, and re-layouts, figure_plan(): jnp.split(mine_x, lax.axis_size('rows'), 1)  5.01 us
    and x8, local copies, waits for them, and re-layouts, unpack(): jnp.bitwise_and(jnp.right_shift(words, 8 * k), 255)  3.23 us
  transfers between devices with their start and end apart: 1, of which 0 were waited for; matrix products, arithmetic and copies ran while one was open for 0% of the time, Pallas kernels for 0%

profile of v1, /device:TPU:0, one launch (start us, length us, event | category | flops | bytes accessed | tf_op | source)
XLA Modules:
  0.0 96.1 jit_solution(671744445005483780)
XLA Ops:
  0.0 5.0 %fusion.13 = (s32[1024,16]{1,0:T(8,128)S(1)}, s32[1024,16]{1,0:T(8,128)S(1)}, s32[1024,16]{1,0:T(8,128)S(1)}, s32[1024,16]{1,0:T(8,128)S(1)}, s32[1024,16]{1,0:T...) fusion(s32[1024,128]{1,0:T(8,128)} %param.5), kind=kLoop, calls=%fused_computation.35 | loop fusion | bytes 1048576 | tf_op jit(solution)/shard_map/split | solution.py:51
  5.0 1.2 %copy.65 = s32[1024,16]{0,1:T(8,128)S(1)} copy(s32[1024,16]{1,0:T(8,128)} %get-tuple-element.108) | data formatting | bytes 131072
  6.2 0.6 bitcast_dynamic-update-slice_fusion.7
  6.8 1.2 %copy.66 = s32[1024,16]{0,1:T(8,128)S(1)} copy(s32[1024,16]{1,0:T(8,128)} %get-tuple-element.107) | data formatting | bytes 131072
  8.1 0.2 copy.67
  8.2 0.2 copy.68
  8.4 0.0 copy-start
  8.4 0.2 copy.69
  8.6 0.2 copy.70
  8.7 0.2 copy.71
  8.9 0.2 copy.72
  9.1 0.6 bitcast_dynamic-update-slice_fusion.6
  9.7 0.6 bitcast_dynamic-update-slice_fusion.5
  10.3 0.6 bitcast_dynamic-update-slice_fusion.4
  11.0 0.6 bitcast_dynamic-update-slice_fusion.3
  11.6 0.6 bitcast_dynamic-update-slice_fusion.2
  12.2 0.6 bitcast_dynamic-update-slice_fusion.1
  12.8 0.6 bitcast_dynamic-update-slice_fusion
  13.5 5.2 %all-to-all-start = ((s32[8,1024,16]{1,2,0:T(8,128)}), s32[8,1024,16]{1,2,0:T(8,128)S(1)}, u32[]{:S(2)}, u32[]{:S(2)}) async-start(s32[8,1024,16]{1,2,0:T(8,128)} %bitcast_dynamic-update-slice_fusion), calls=%async_computation | async-start | bytes 1048576 | tf_op jit(solution)/shard_map/all_to_all | solution.py:51
  18.7 0.0 copy-done
  18.7 13.2 %all_gather.6 = f32[32768]{0:T(1024)S(1)} all-gather(f32[4096]{0:T(1024)S(1)} %copy-done), channel_id=1, replica_groups=mesh['rows'=8,'feat'=4] {'rows'}, dimensions={0}, use_global_device_ids=true | all-gather | bytes 147456 | tf_op jit(solution)/shard_map/all_gather | solution.py:55
  31.9 0.0 all-to-all-done
  31.9 0.3 shift-right-arithmetic_and_fusion.3
  32.2 0.3 copy.57
  32.5 0.1 and.63
  32.6 0.3 copy.58
  32.9 0.1 and.65
  33.0 0.3 copy.59
  33.3 0.9 and.67
  34.2 0.3 copy.60
  34.5 0.9 and.69
  35.4 1.3 %pad_add_fusion = s32[8192,4,16]{0,2,1:T(8,128)S(1)} fusion(s32[8192,1,16]{0,2,1:T(8,128)} %and.69, s32[8192,1,16]{0,2,1:T(8,128)} %and.67, s32[8192,1,16]{0,2,1:T(8,128)S(1)} %and.65, s32[8192,1,16]{0,2,1:T(8,128)S(1)} %and.63), kind=kLoop, calls=%fused_computation.14 | loop fusion | flops 1572864 | bytes 4194304 | tf_op jit(solution)/shard_map/stack | solution.py:12
  36.8 10.7 %copy.61 = s32[8192,4,16]{2,1,0:T(4,128)} copy(s32[8192,4,16]{0,2,1:T(8,128)S(1)} %pad_add_fusion) | data formatting | bytes 4194304 | tf_op jit(solution)/shard_map/stack | solution.py:12
  47.5 9.6 %copy.62 = s32[8,4096,16]{1,2,0:T(8,128)S(1)} copy(s32[8,4096,16]{2,1,0:T(8,128)} %bitcast.42) | data formatting | bytes 4194304
  57.1 0.0 copy-start.1
  57.1 27.9 %while.12 = (s32[]{:T(128)}, f32[16,16,16]{2,1,0:T(8,128)S(1)}, s32[8,4096,16]{1,2,0:T(8,128)S(1)}, f32[8,4096]{1,0:T(8,128)S(1)}, s32[]{:T(128)}, /*index=5*/s32[]{:T(128)}) while((s32[]{:T(128)}, f32[16,16,16]{2,1,0:T(8,128)S(1)}, s32[8,4096,16]{1,2,0:T(8,128)S(1)}, f32[8,4096]{1,0:T(8,128)S(1)}, s32[]{:T(128)}, ...), condition=%wide.region_1.2_spmd.clone.clone, body=%wide.region_0.1_spmd.clone.clone.sunk | while | flops 204611584 | bytes 1392727 | solution.py:34
  57.2 3.4 %fusion.17 = f32[16,16,16]{2,1,0:T(8,128)S(1)} fusion(s32[4096,16]{0,1:T(8,128)S(1)} %get-tuple-element.138, f32[4096]{0:T(1024)S(1)} %bitcast.43, s32[4096,16]{0,1:T(8,128)S(1)} %get-tuple-element.139, f32[16,16,16]{2,1,0:T(8,128)S(1)} %get-tuple-element.147, pred[]{:T(512)S(6)} %compare.3), kind=kOutput, calls=%fused_computation.9.clone.1 | convolution fusion | flops 204480512 | bytes 573441 | tf_op jit(solution)/shard_map/while/body/eval_jaxpr/rkh,rkl->khl/dot_general | solution.py:30
  60.7 3.4 %fusion.17 = f32[16,16,16]{2,1,0:T(8,128)S(1)} fusion(s32[4096,16]{0,1:T(8,128)S(1)} %get-tuple-element.138, f32[4096]{0:T(1024)S(1)} %bitcast.43, s32[4096,16]{0,1:T(8,128)S(1)} %get-tuple-element.139, f32[16,16,16]{2,1,0:T(8,128)S(1)} %get-tuple-element.147, pred[]{:T(512)S(6)} %compare.3), kind=kOutput, calls=%fused_computation.9.clone.1 | convolution fusion | flops 204480512 | bytes 573441 | tf_op jit(solution)/shard_map/while/body/eval_jaxpr/rkh,rkl->khl/dot_general | solution.py:30
  64.2 3.4 %fusion.17 = f32[16,16,16]{2,1,0:T(8,128)S(1)} fusion(s32[4096,16]{0,1:T(8,128)S(1)} %get-tuple-element.138, f32[4096]{0:T(1024)S(1)} %bitcast.43, s32[4096,16]{0,1:T(8,128)S(1)} %get-tuple-element.139, f32[16,16,16]{2,1,0:T(8,128)S(1)} %get-tuple-element.147, pred[]{:T(512)S(6)} %compare.3), kind=kOutput, calls=%fused_computation.9.clone.1 | convolution fusion | flops 204480512 | bytes 573441 | tf_op jit(solution)/shard_map/while/body/eval_jaxpr/rkh,rkl->khl/dot_general | solution.py:30
  67.7 3.4 %fusion.17 = f32[16,16,16]{2,1,0:T(8,128)S(1)} fusion(s32[4096,16]{0,1:T(8,128)S(1)} %get-tuple-element.138, f32[4096]{0:T(1024)S(1)} %bitcast.43, s32[4096,16]{0,1:T(8,128)S(1)} %get-tuple-element.139, f32[16,16,16]{2,1,0:T(8,128)S(1)} %get-tuple-element.147, pred[]{:T(512)S(6)} %compare.3), kind=kOutput, calls=%fused_computation.9.clone.1 | convolution fusion | flops 204480512 | bytes 573441 | tf_op jit(solution)/shard_map/while/body/eval_jaxpr/rkh,rkl->khl/dot_general | solution.py:30
  71.2 3.4 %fusion.17 = f32[16,16,16]{2,1,0:T(8,128)S(1)} fusion(s32[4096,16]{0,1:T(8,128)S(1)} %get-tuple-element.138, f32[4096]{0:T(1024)S(1)} %bitcast.43, s32[4096,16]{0,1:T(8,128)S(1)} %get-tuple-element.139, f32[16,16,16]{2,1,0:T(8,128)S(1)} %get-tuple-element.147, pred[]{:T(512)S(6)} %compare.3), kind=kOutput, calls=%fused_computation.9.clone.1 | convolution fusion | flops 204480512 | bytes 573441 | tf_op jit(solution)/shard_map/while/body/eval_jaxpr/rkh,rkl->khl/dot_general | solution.py:30
  74.7 3.4 %fusion.17 = f32[16,16,16]{2,1,0:T(8,128)S(1)} fusion(s32[4096,16]{0,1:T(8,128)S(1)} %get-tuple-element.138, f32[4096]{0:T(1024)S(1)} %bitcast.43, s32[4096,16]{0,1:T(8,128)S(1)} %get-tuple-element.139, f32[16,16,16]{2,1,0:T(8,128)S(1)} %get-tuple-element.147, pred[]{:T(512)S(6)} %compare.3), kind=kOutput, calls=%fused_computation.9.clone.1 | convolution fusion | flops 204480512 | bytes 573441 | tf_op jit(solution)/shard_map/while/body/eval_jaxpr/rkh,rkl->khl/dot_general | solution.py:30
  78.1 3.4 %fusion.17 = f32[16,16,16]{2,1,0:T(8,128)S(1)} fusion(s32[4096,16]{0,1:T(8,128)S(1)} %get-tuple-element.138, f32[4096]{0:T(1024)S(1)} %bitcast.43, s32[4096,16]{0,1:T(8,128)S(1)} %get-tuple-element.139, f32[16,16,16]{2,1,0:T(8,128)S(1)} %get-tuple-element.147, pred[]{:T(512)S(6)} %compare.3), kind=kOutput, calls=%fused_computation.9.clone.1 | convolution fusion | flops 204480512 | bytes 573441 | tf_op jit(solution)/shard_map/while/body/eval_jaxpr/rkh,rkl->khl/dot_general | solution.py:30
  81.6 3.4 %fusion.17 = f32[16,16,16]{2,1,0:T(8,128)S(1)} fusion(s32[4096,16]{0,1:T(8,128)S(1)} %get-tuple-element.138, f32[4096]{0:T(1024)S(1)} %bitcast.43, s32[4096,16]{0,1:T(8,128)S(1)} %get-tuple-element.139, f32[16,16,16]{2,1,0:T(8,128)S(1)} %get-tuple-element.147, pred[]{:T(512)S(6)} %compare.3), kind=kOutput, calls=%fused_computation.9.clone.1 | convolution fusion | flops 204480512 | bytes 573441 | tf_op jit(solution)/shard_map/while/body/eval_jaxpr/rkh,rkl->khl/dot_general | solution.py:30
  85.0 0.1 reshape.159
  85.1 0.1 reshape.161
  85.3 0.6 reduce-window.6
  85.9 0.2 slice_reduce_fusion
  86.1 0.1 copy_bitcast_fusion
  86.1 0.2 slice_reduce_fusion.1
  86.3 0.1 fusion.12
  86.4 0.0 copy-done.1
  86.4 0.1 broadcast_multiply_fusion
  86.5 0.7 clamp_reduce_fusion
  87.2 8.3 %all_gather.7 = f32[128,128]{1,0:T(8,128)S(1)} all-gather(f32[16,128]{1,0:T(8,128)S(1)} %clamp_reduce_fusion), channel_id=1, replica_groups=mesh['rows'=8,'feat'=4] {'rows'}, dimensions={0}, use_global_device_ids=true | all-gather | bytes 73728 | tf_op jit(solution)/shard_map/all_gather | solution.py:58
  95.4 0.6 copy.91
  (21 shorter events, 0.6 us)
Async XLA Ops:
  8.4 10.3 %copy-start = (f32[4096]{0:T(1024)S(1)}, f32[4096]{0:T(1024)}, u32[]{:S(2)}) copy-start(f32[4096]{0:T(1024)} %param.6) | copy-start | bytes 49156
  13.5 18.4 %all-to-all-start = ((s32[8,1024,16]{1,2,0:T(8,128)}), s32[8,1024,16]{1,2,0:T(8,128)S(1)}, u32[]{:S(2)}, u32[]{:S(2)}) async-start(s32[8,1024,16]{1,2,0:T(8,128)} %bitcast_dynamic-update-slice_fusion), calls=%async_computation | async-start | bytes 1048576 | tf_op jit(solution)/shard_map/all_to_all | solution.py:51
  57.1 29.3 %copy-start.1 = (f32[128]{0:T(128)S(1)}, f32[128]{0:T(128)}, u32[]{:S(2)}) copy-start(f32[128]{0:T(128)} %param.7) | copy-start | bytes 1540
